TPU v7x, 32 devices: a whole 2x2x4 slice. The times are simulated.
32 devices in a mesh: bl: 8 (over z, x), tm: 4 (over y, core).
Axes of the slice: x: 2, y: 2, z: 4, core: 2. Of those that a mesh axis runs over, the one named last changes fastest.
Arguments:
- visibility_real: bfloat16 [3072, 16, 1024], P('bl', 'tm'), may hold values from -6 to 6
- visibility_imag: bfloat16 [3072, 16, 1024], P('bl', 'tm'), may hold values from -6 to 6
- weights: int32 [3072, 16], P('bl', 'tm'), may hold values from 0 to 8
- labels: int32 [3072], P('bl'), may hold values from 0 to 511, as said below
- owner_of: int32 [512], replicated, may hold values from 0 to 7, as said below
Outputs:
- bandpower: float32 [512, 1024], P(('bl', 'tm'))
Inputs may be any that keep to these rules, and one draw needn't show every extreme that they name: Of the rows of one device, at most 72 have labels of groups with one owner, and these carry at most 18 different labels; in every draw some owner gets exactly 72 such rows with exactly 18 labels from every device. `owner_of`: every owner owns exactly 64 groups.
All inputs are finite; a program needn't handle non-finite values.
Results may differ from a plain program's by a relative error of at most 0.0003.
Values may be sent and summed in bfloat16 or wider, within the bound.
A program may use at most 128 MiB of HBM per device.

v0:
```python
import math

import jax
import jax.numpy as jnp
from jax import lax
from jax.sharding import PartitionSpec as P

HARRIS = (0.35875, 0.48829, 0.14128, 0.01168)


def from_behind(block, axis, distance):
    devices = range(lax.axis_size(axis))
    route = [(i - distance, i) for i in devices if i - distance in devices]
    return lax.ppermute(block, axis, route)


def taper_of(length):
    phase_angle = 2.0 * math.pi / length * jnp.arange(length, dtype=jnp.float32)
    return (
        HARRIS[0]
        - HARRIS[1] * jnp.cos(phase_angle)
        + HARRIS[2] * jnp.cos(2.0 * phase_angle)
        - HARRIS[3] * jnp.cos(3.0 * phase_angle)
    )


def dft_tables(channels):
    window_taper = taper_of(channels)
    window_taper = window_taper / jnp.sqrt(jnp.sum(window_taper * window_taper))
    channel_index = jnp.arange(channels, dtype=jnp.int32)
    phase_turns = channel_index[:, None] * channel_index[None, :] % channels
    phase_angle = 2.0 * math.pi / channels * phase_turns.astype(jnp.float32)
    cosine = jnp.cos(phase_angle) * window_taper[:, None]
    sine_part = jnp.sin(phase_angle) * window_taper[:, None]
    table_real = jnp.concatenate([cosine, -sine_part], axis=1)
    table_imag = jnp.concatenate([sine_part, cosine], axis=1)
    return (table_real, table_imag)


def owner_rank(owner_of, owners):
    owner_hits = (owner_of[:, None] == jnp.arange(owners, dtype=jnp.int32)[None, :]).astype(
        jnp.int32
    )
    earlier = jnp.cumsum(owner_hits, axis=0) - owner_hits
    return jnp.sum(earlier * owner_hits, axis=1)


def per_device(visibility_real, visibility_imag, weights, labels, owner_of):
    row_count, resident_times, channels = visibility_real.shape
    owners = lax.axis_size("bl")
    groups = owner_of.shape[0]
    per_owner = groups // owners
    capacity = 3 * row_count // (2 * owners)
    distinct = min(capacity // 4, per_owner // 2)
    table_real, table_imag = dft_tables(channels)
    group_rank = owner_rank(owner_of, owners)
    label_match = labels[:, None] == jnp.arange(groups, dtype=jnp.int32)[None, :]
    row_owner = jnp.sum(jnp.where(label_match, owner_of[None, :], 0), axis=1)
    row_rank = jnp.sum(jnp.where(label_match, group_rank[None, :], 0), axis=1)
    group_index = jnp.arange(per_owner, dtype=jnp.int32)[:, None, None]
    local_key = row_owner * per_owner + row_rank
    key_match = local_key[:, None] == jnp.arange(groups, dtype=jnp.int32)[None, :]
    present = jnp.any(key_match, axis=0).astype(jnp.int32).reshape(owners, per_owner)
    order_within = jnp.cumsum(present, axis=1) - present
    slot_of_key = (jnp.arange(owners, dtype=jnp.int32)[:, None] * distinct + order_within).reshape(
        groups
    )
    row_slot = jnp.sum(jnp.where(key_match, slot_of_key[None, :], 0), axis=1)
    slot_hit = (
        order_within[:, :, None] == jnp.arange(distinct, dtype=jnp.int32)[None, None, :]
    ) & (present[:, :, None] > 0)
    slot_rank = jnp.sum(
        jnp.where(slot_hit, jnp.arange(per_owner, dtype=jnp.int32)[None, :, None], 0), axis=1
    )
    send_rank = jnp.broadcast_to(slot_rank[:, :, None], (owners, distinct, resident_times))
    slot_weight = jnp.where(
        row_slot[None, :, None] == jnp.arange(owners * distinct, dtype=jnp.int32)[:, None, None],
        weights[None],
        0,
    )
    folder = slot_weight.astype(jnp.bfloat16)
    part_real = jnp.einsum(
        "krt,rtf->ktf", folder, visibility_real, preferred_element_type=jnp.float32
    ).reshape(owners, distinct, resident_times, channels)
    part_imag = jnp.einsum(
        "krt,rtf->ktf", folder, visibility_imag, preferred_element_type=jnp.float32
    ).reshape(owners, distinct, resident_times, channels)
    part_weight = (
        jnp.sum(slot_weight, axis=1).astype(jnp.float32).reshape(owners, distinct, resident_times)
    )
    received_real = lax.all_to_all(part_real, "bl", split_axis=0, concat_axis=0, tiled=True)
    came_imag = lax.all_to_all(part_imag, "bl", split_axis=0, concat_axis=0, tiled=True)
    came_weight = lax.all_to_all(part_weight, "bl", split_axis=0, concat_axis=0, tiled=True)
    came_rank = lax.all_to_all(send_rank, "bl", split_axis=0, concat_axis=0, tiled=True)
    items = received_real.shape[2]
    flat_real = received_real.reshape(-1, items, channels)
    flat_imag = came_imag.reshape(-1, items, channels)
    flat_weight = came_weight.reshape(-1, items)
    flat_rank = came_rank.reshape(-1, items)
    selector = (flat_rank[None] == group_index).astype(jnp.float32)
    sum_real = jnp.einsum("gsn,snf->gnf", selector, flat_real, precision=lax.Precision.HIGHEST)
    sum_imag = jnp.einsum("gsn,snf->gnf", selector, flat_imag, precision=lax.Precision.HIGHEST)
    weight_sum = jnp.sum(selector * flat_weight[None], axis=1)
    divisor = jnp.maximum(weight_sum, 1.0)[:, :, None]
    mean_real = sum_real / divisor
    mean_imag = sum_imag / divisor
    arrived_result = jnp.einsum(
        "gnf,fk->gnk", mean_real, table_real, precision=lax.Precision.HIGHEST
    ) + jnp.einsum("gnf,fk->gnk", mean_imag, table_imag, precision=lax.Precision.HIGHEST)
    following = from_behind(arrived_result[:, 0, :], "tm", -1)
    pair_sum = (
        jnp.sum(arrived_result[:, :-1, :] * arrived_result[:, 1:, :], axis=1)
        + arrived_result[:, -1, :] * following
    )
    partial_power = pair_sum[:, :channels] + pair_sum[:, channels:]
    return lax.psum_scatter(partial_power, "tm", scatter_dimension=0, tiled=True)


def solution(mesh):
    placed = (P("bl", "tm", None), P("bl", "tm", None), P("bl", "tm"), P("bl"), P())
    return jax.shard_map(
        per_device, mesh=mesh, in_specs=placed, out_specs=P(("bl", "tm"), None), check_vma=False
    )
```

profile of v0, /device:TPU:1, one launch (start us, length us, event | category | flops | bytes accessed | tf_op | source)
XLA Modules:
  0.0 207.6 jit_solution(15908951253186228510)
XLA Ops:
  6.5 0.8 fusion.55
  7.4 1.1 reduce-window.6
  8.5 0.2 slice_reduce_fusion
  8.8 0.8 fusion.54
  9.5 1.1 select_reduce_fusion.3
  10.6 0.2 fusion.41
  10.8 0.1 reshape.131
  10.9 0.2 reduce_window_sum.30
  11.1 0.4 select_reduce_fusion.5
  11.5 0.1 copy.25
  11.6 0.6 broadcast_in_dim.92
  12.2 6.3 %all-to-all-start.1 = ((s32[8,18,4]{1,2,0:T(4,128)}), s32[8,18,4]{1,2,0:T(4,128)S(1)}, u32[]{:S(2)}, u32[]{:S(2)}) async-start(s32[8,18,4]{1,2,0:T(4,128)} %broadcast_in_dim.92), calls=%async_computation.1 | async-start | bytes 32768 | tf_op jit(solution)/shard_map/all_to_all | solution.py:94
  18.5 0.1 reduce_window_sum.31
  18.6 0.1 add.50
  18.7 0.1 add.51
  18.8 0.2 select_reduce_fusion.1
  19.0 0.9 select_reduce_fusion
  20.0 0.1 convert_element_type.51
  20.1 0.6 copy.28
  20.7 3.3 %all-to-all-done.1 = s32[8,18,4]{1,2,0:T(4,128)S(1)} async-done(((s32[8,18,4]{1,2,0:T(4,128)}), s32[8,18,4]{1,2,0:T(4,128)S(1)}, u32[]{:S(2)}, u32[]{:S(2)}) %all-to-all-start.1) | async-done | bytes 2336 | tf_op jit(solution)/shard_map/all_to_all | solution.py:94
  24.0 3.3 %all-to-all-start.2 = ((f32[8,18,4]{1,2,0:T(4,128)}), f32[8,18,4]{1,2,0:T(4,128)S(1)}, u32[]{:S(2)}, u32[]{:S(2)}) async-start(f32[8,18,4]{1,2,0:T(4,128)} %copy.28), calls=%async_computation.2 | async-start | bytes 32768 | tf_op jit(solution)/shard_map/all_to_all | solution.py:93
  27.3 2.8 %fusion.21 = f32[144,4,1024]{2,0,1:T(8,128)S(1)} fusion(bf16[384,4,1024]{2,1,0:T(4,128)(2,1)S(1)} %copy-done, s32[384,4]{0,1:T(4,128)} %param.7, pred[144,384]{1,0:T(8,128)(4,1)S(1)} %iota_compare_fusion.5), kind=kOutput, calls=%fused_computation.28 | convolution fusion | flops 453427200 | bytes 5566464 | tf_op jit(solution)/shard_map/krt,rtf->ktf/dot_general | solution.py:82
  30.2 0.0 copy-start.3
  30.2 2.9 %copy.24 = f32[144,4,1024]{2,1,0:T(4,128)} copy(f32[144,4,1024]{2,0,1:T(8,128)S(1)} %fusion.21) | data formatting | bytes 4718592 | tf_op jit(solution)/shard_map/krt,rtf->ktf/transpose | solution.py:82
  33.1 5.4 %all-to-all-start = ((f32[8,18,4,1024]{3,2,1,0:T(4,128)}), f32[8,18,4,1024]{3,2,1,0:T(4,128)}, u32[]{:S(2)}, u32[]{:S(2)}) async-start(f32[8,18,4,1024]{3,2,1,0:T(4,128)} %bitcast.50), calls=%async_computation | async-start | bytes 4718592 | tf_op jit(solution)/shard_map/all_to_all | solution.py:91
  38.5 4.1 %fusion.24 = f32[144,4,1024]{2,0,1:T(8,128)S(1)} fusion(bf16[384,4,1024]{2,1,0:T(4,128)(2,1)} %param.6, s32[384,4]{0,1:T(4,128)S(1)} %copy-done.3, pred[144,384]{1,0:T(8,128)(4,1)S(1)} %iota_compare_fusion.5), kind=kOutput, calls=%fused_computation.29 | convolution fusion | flops 453427200 | bytes 5566464 | tf_op jit(solution)/shard_map/krt,rtf->ktf/dot_general | solution.py:85
  42.5 2.9 %copy.31 = f32[144,4,1024]{2,1,0:T(4,128)} copy(f32[144,4,1024]{2,0,1:T(8,128)S(1)} %fusion.24) | data formatting | bytes 4718592 | tf_op jit(solution)/shard_map/krt,rtf->ktf/transpose | solution.py:85
  45.5 44.5 %all-to-all-done = f32[8,18,4,1024]{3,2,1,0:T(4,128)} async-done(((f32[8,18,4,1024]{3,2,1,0:T(4,128)}), f32[8,18,4,1024]{3,2,1,0:T(4,128)}, u32[]{:S(2)}, u32[]{:S(2)}) %all-to-all-start) | async-done | bytes 2359328 | tf_op jit(solution)/shard_map/all_to_all | solution.py:91
  89.9 6.3 %all-to-all-start.3 = ((f32[8,18,4,1024]{3,2,1,0:T(4,128)}), f32[8,18,4,1024]{3,2,1,0:T(4,128)}, u32[]{:S(2)}, u32[]{:S(2)}) async-start(f32[8,18,4,1024]{3,2,1,0:T(4,128)} %bitcast.49), calls=%async_computation.3 | async-start | bytes 4718592 | tf_op jit(solution)/shard_map/all_to_all | solution.py:92
  96.3 0.2 reduce-scatter.2.cloned.1.call-start
  96.5 0.7 multiply_reduce_fusion
  97.8 0.1 fusion.65
  97.9 19.6 %sine_multiply_fusion = (f32[1024,1024]{1,0:T(8,128)}, f32[1024,1024]{1,0:T(8,128)}, f32[1024,1024]{1,0:T(8,128)}) fusion(f32[1024]{0:T(1024)S(1)} %fusion.65), kind=kLoop, calls=%fused_computation.14 | loop fusion | flops 17825792 | bytes 12587008 | tf_op jit(solution)/shard_map/mul | solution.py:34
  117.5 0.1 eq.116
  117.5 0.1 mul.157
  117.6 0.1 select_reduce_fusion.4
  117.8 4.8 %fusion.38 = f32[64,4,1024]{2,0,1:T(8,128)} fusion(f32[144,4,1024]{2,1,0:T(4,128)} %bitcast.5, f32[64,4]{0,1:T(4,128)S(1)} %broadcast_maximum_fusion, s32[144,4]{0,1:T(4,128)S(1)} %eq.116), kind=kOutput, calls=%fused_computation.36 | convolution fusion | flops 453283840 | bytes 3411200 | tf_op jit(solution)/shard_map/gsn,snf->gnf/dot_general | solution.py:101
  122.6 26.4 %all-to-all-done.3 = f32[8,18,4,1024]{3,2,1,0:T(4,128)} async-done(((f32[8,18,4,1024]{3,2,1,0:T(4,128)}), f32[8,18,4,1024]{3,2,1,0:T(4,128)}, u32[]{:S(2)}, u32[]{:S(2)}) %all-to-all-start.3) | async-done | bytes 2359328 | tf_op jit(solution)/shard_map/all_to_all | solution.py:92
  149.0 4.0 %fusion.35 = f32[64,4,1024]{2,0,1:T(8,128)S(1)} fusion(f32[144,4,1024]{2,1,0:T(4,128)} %bitcast.10, f32[64,4]{0,1:T(4,128)S(1)} %broadcast_maximum_fusion, s32[144,4]{0,1:T(4,128)S(1)} %eq.116), kind=kOutput, calls=%fused_computation.35 | convolution fusion | flops 453283840 | bytes 3411200 | tf_op jit(solution)/shard_map/gsn,snf->gnf/dot_general | solution.py:102
  153.0 9.6 %fusion = f32[64,4,2048]{2,0,1:T(8,128)S(1)} fusion(f32[64,4,1024]{2,0,1:T(8,128)} %fusion.38, f32[1024,1024]{1,0:T(8,128)} %get-tuple-element.8, f32[1024,1024]{1,0:T(8,128)S(1)} %copy-done.1), kind=kOutput, calls=%fused_computation.1 | convolution fusion | flops 6444548096 | bytes 11534336 | tf_op jit(solution)/shard_map/gnf,fk->gnk/dot_general | solution.py:107
  162.6 7.4 %fusion.16 = f32[64,4,2048]{2,0,1:T(8,128)S(1)} fusion(f32[64,4,2048]{2,0,1:T(8,128)S(1)} %fusion, f32[64,4,1024]{2,0,1:T(8,128)S(1)} %fusion.35, f32[1024,1024]{1,0:T(8,128)S(1)} %copy-done.1, f32[1024,1024]{1,0:T(8,128)S(1)} %copy-done.2), kind=kOutput, calls=%fused_computation.23 | convolution fusion | flops 6445072384 | bytes 13631488 | tf_op jit(solution)/shard_map/gnf,fk->gnk/dot_general | solution.py:109
  170.1 4.1 %collective-permute-start = (f32[64,2048]{1,0:T(8,128)S(1)}, f32[64,2048]{1,0:T(8,128)S(1)}, u32[]{:S(2)}, u32[]{:S(2)}) collective-permute-start(f32[64,2048]{1,0:T(8,128)S(1)} %slice_bitcast_fusion), channel_id=1, source_target_pairs={{1,0},{2,1},{3,2},{5,4},{6,5},{7,6},{9,8},{10,9},{11,10},{13,12},{... | collective-permute-start | bytes 1572872 | tf_op jit(solution)/shard_map/ppermute | solution.py:14
  174.2 0.2 fusion.28
  174.4 7.7 %collective-permute-done = f32[64,2048]{1,0:T(8,128)S(1)} collective-permute-done((f32[64,2048]{1,0:T(8,128)S(1)}, f32[64,2048]{1,0:T(8,128)S(1)}, u32[]{:S(2)}, u32[]{:S(2)}) %collective-permute-start) | collective-permute-done | bytes 524320 | tf_op jit(solution)/shard_map/ppermute | solution.py:14
  182.2 0.1 fusion.43
  182.3 0.7 slice_add_fusion
  183.0 0.0 reduce-scatter.2.cloned.1.call-update
  183.0 17.7 %reduce-scatter.2.cloned.1.call-done = f32[16,1024]{1,0:T(8,128)} async-done(((f32[64,1024]{1,0:T(8,128)}), f32[16,1024]{1,0:T(8,128)}) %reduce-scatter.2.cloned.1.call-update) | async-done | bytes 65552 | tf_op jit(solution)/shard_map/reduce_scatter | solution.py:116
  (22 shorter events, 0.2 us)
Async XLA Ops:
  6.5 20.8 %copy-start = (bf16[384,4,1024]{2,1,0:T(4,128)(2,1)S(1)}, bf16[384,4,1024]{2,1,0:T(4,128)(2,1)}, u32[]{:S(2)}) copy-start(bf16[384,4,1024]{2,1,0:T(4,128)(2,1)} %param.5) | copy-start | bytes 9437188
  12.2 11.8 %all-to-all-start.1 = ((s32[8,18,4]{1,2,0:T(4,128)}), s32[8,18,4]{1,2,0:T(4,128)S(1)}, u32[]{:S(2)}, u32[]{:S(2)}) async-start(s32[8,18,4]{1,2,0:T(4,128)} %broadcast_in_dim.92), calls=%async_computation.1 | async-start | bytes 32768 | tf_op jit(solution)/shard_map/all_to_all | solution.py:94
  24.0 9.2 %all-to-all-start.2 = ((f32[8,18,4]{1,2,0:T(4,128)}), f32[8,18,4]{1,2,0:T(4,128)S(1)}, u32[]{:S(2)}, u32[]{:S(2)}) async-start(f32[8,18,4]{1,2,0:T(4,128)} %copy.28), calls=%async_computation.2 | async-start | bytes 32768 | tf_op jit(solution)/shard_map/all_to_all | solution.py:93
  30.2 8.3 %copy-start.3 = (s32[384,4]{0,1:T(4,128)S(1)}, s32[384,4]{0,1:T(4,128)}, u32[]{:S(2)}) copy-start(s32[384,4]{0,1:T(4,128)} %param.7) | copy-start | bytes 18436
  33.1 56.8 %all-to-all-start = ((f32[8,18,4,1024]{3,2,1,0:T(4,128)}), f32[8,18,4,1024]{3,2,1,0:T(4,128)}, u32[]{:S(2)}, u32[]{:S(2)}) async-start(f32[8,18,4,1024]{3,2,1,0:T(4,128)} %bitcast.50), calls=%async_computation | async-start | bytes 4718592 | tf_op jit(solution)/shard_map/all_to_all | solution.py:91
  89.9 59.1 %all-to-all-start.3 = ((f32[8,18,4,1024]{3,2,1,0:T(4,128)}), f32[8,18,4,1024]{3,2,1,0:T(4,128)}, u32[]{:S(2)}, u32[]{:S(2)}) async-start(f32[8,18,4,1024]{3,2,1,0:T(4,128)} %bitcast.49), calls=%async_computation.3 | async-start | bytes 4718592 | tf_op jit(solution)/shard_map/all_to_all | solution.py:92
  96.3 104.5 %reduce-scatter.2.cloned.1.call-start = ((), (), s32[]{:S(2)}) async-start(), calls=%async_computation.5 | async-start | bytes 327680 | tf_op jit(solution)/shard_map/reduce_scatter | solution.py:116
  149.0 4.0 %copy-start.1 = (f32[1024,1024]{1,0:T(8,128)S(1)}, f32[1024,1024]{1,0:T(8,128)}, u32[]{:S(2)}) copy-start(f32[1024,1024]{1,0:T(8,128)} %get-tuple-element.9) | copy-start | bytes 12582916
  153.0 9.6 %copy-start.2 = (f32[1024,1024]{1,0:T(8,128)S(1)}, f32[1024,1024]{1,0:T(8,128)}, u32[]{:S(2)}) copy-start(f32[1024,1024]{1,0:T(8,128)} %get-tuple-element.7) | copy-start | bytes 12582916
  170.1 12.1 %collective-permute-start = (f32[64,2048]{1,0:T(8,128)S(1)}, f32[64,2048]{1,0:T(8,128)S(1)}, u32[]{:S(2)}, u32[]{:S(2)}) collective-permute-start(f32[64,2048]{1,0:T(8,128)S(1)} %slice_bitcast_fusion), channel_id=1, source_target_pairs={{1,0},{2,1},{3,2},{5,4},{6,5},{7,6},{9,8},{10,9},{11,10},{13,12},{... | collective-permute-start | bytes 1572872 | tf_op jit(solution)/shard_map/ppermute | solution.py:14
Sparse Core Ops, SparseCore 0:
  183.2 17.5 reduce-scatter.1
where the time goes:
time: 209 us; the launch traced here: 208 us
  waiting for transfers between devices  99.6 us (48%)
  matrix products  32.7 us (16%)
  other arithmetic  27.3 us (13%)
  starting transfers between devices  25.7 us (12%)
  between operations  14.3 us (7%)
  local copies, waits for them, and re-layouts  7.98 us (4%)
    all_to_all x1, waiting for transfers between devices, per_device(): lax.all_to_all(part_real, 'bl', split_axis=0, concat_axis=0, tiled=True)  44.5 us
    all_to_all x1, waiting for transfers between devices, per_device(): lax.all_to_all(part_imag, 'bl', split_axis=0, concat_axis=0, tiled=True)  26.4 us
    mul x1, other arithmetic, dft_tables(): sine_part = jnp.sin(phase_angle) * window_taper[:, None]  19.6 us
    reduce_scatter x1, waiting for transfers between devices, per_device(): lax.psum_scatter(partial_power, 'tm', scatter_dimension=0, tiled=True)  17.7 us
    dot_general x1, matrix products, per_device(): jnp.einsum('gnf,fk->gnk', mean_real, table_real, precision=lax.Precision....  9.61 us
    ppermute x1, waiting for transfers between devices, from_behind(): return lax.ppermute(block, axis, route)  7.75 us
    dot_general x1, matrix products, per_device(): jnp.einsum('gnf,fk->gnk', mean_imag, table_imag, precision=lax.Precision....  7.4 us
    all_to_all x1, starting transfers between devices, per_device(): lax.all_to_all(send_rank, 'bl', split_axis=0, concat_axis=0, tiled=True)  6.34 us
  transfers between devices with their start and end apart: 6, of which 5 were waited for; matrix products, arithmetic and copies ran while one was open for 20% of the time, Pallas kernels for 0%

commit v1 on v0

v1 whole, which is shorter than its diff:
```python
import math

import jax
import jax.numpy as jnp
from jax import lax
from jax.sharding import PartitionSpec as P

HARRIS = (0.35875, 0.48829, 0.14128, 0.01168)
RADIX = 4


def taper_of(length):
    phase_angle = 2.0 * math.pi / length * jnp.arange(length, dtype=jnp.float32)
    taper = (
        HARRIS[0]
        - HARRIS[1] * jnp.cos(phase_angle)
        + HARRIS[2] * jnp.cos(2.0 * phase_angle)
        - HARRIS[3] * jnp.cos(3.0 * phase_angle)
    )
    return taper / jnp.sqrt(jnp.sum(taper * taper))


def dft_table(channels):
    short = channels // RADIX
    residue = jnp.arange(RADIX, dtype=jnp.int32)[:, None, None]
    row = jnp.arange(short, dtype=jnp.int32)[None, :, None]
    column = jnp.arange(short, dtype=jnp.int32)[None, None, :]
    turns = row * (RADIX * column + residue) % channels
    angle = 2.0 * math.pi / channels * turns.astype(jnp.float32)
    cosine, sine = jnp.cos(angle), jnp.sin(angle)
    top = jnp.concatenate([cosine, -sine], axis=2)
    bottom = jnp.concatenate([sine, cosine], axis=2)
    return jnp.concatenate([top, bottom], axis=1)


def owner_rank(owner_of, owners):
    hits = (owner_of[:, None] == jnp.arange(owners, dtype=jnp.int32)[None, :]).astype(jnp.int32)
    earlier = jnp.cumsum(hits, axis=0) - hits
    return jnp.sum(earlier * hits, axis=1)


def slots(labels, owner_of, owners, distinct):
    groups = owner_of.shape[0]
    per_owner = groups // owners
    group_rank = owner_rank(owner_of, owners)
    label_match = labels[:, None] == jnp.arange(groups, dtype=jnp.int32)[None, :]
    group_key = owner_of * per_owner + group_rank
    local_key = jnp.sum(jnp.where(label_match, group_key[None, :], 0), axis=1)
    key_match = local_key[:, None] == jnp.arange(groups, dtype=jnp.int32)[None, :]
    present = jnp.any(key_match, axis=0).astype(jnp.int32).reshape(owners, per_owner)
    order_within = jnp.cumsum(present, axis=1) - present
    slot_of_key = (jnp.arange(owners, dtype=jnp.int32)[:, None] * distinct + order_within).reshape(
        groups
    )
    row_slot = jnp.sum(jnp.where(key_match, slot_of_key[None, :], 0), axis=1)
    slot_hit = (
        order_within[:, :, None] == jnp.arange(distinct, dtype=jnp.int32)[None, None, :]
    ) & (present[:, :, None] > 0)
    slot_rank = jnp.sum(
        jnp.where(slot_hit, jnp.arange(per_owner, dtype=jnp.int32)[None, :, None], 0), axis=1
    )
    return row_slot, slot_rank


def per_device(visibility_real, visibility_imag, weights, labels, owner_of):
    row_count, times, channels = visibility_real.shape
    owners = lax.axis_size("bl")
    parts = lax.axis_size("tm")
    groups = owner_of.shape[0]
    per_owner = groups // owners
    capacity = 3 * row_count // (2 * owners)
    distinct = min(capacity // 4, per_owner // 2)
    row_slot, slot_rank = slots(labels, owner_of, owners, distinct)

    sent = distinct * times
    slot_id = jnp.arange(owners * distinct, dtype=jnp.int32)
    same_time = jnp.eye(times, dtype=jnp.int32)
    hit = (row_slot[None, :] == slot_id[:, None]).astype(jnp.int32)
    folder = (
        (hit[:, None, :, None] * (same_time[:, None, :] * weights[None])[None])
        .astype(jnp.bfloat16)
        .reshape(owners * sent, row_count * times)
    )
    part_weight = jnp.sum(hit[:, :, None] * weights[None], axis=1).astype(jnp.float32)
    part_real = jnp.dot(
        folder,
        visibility_real.reshape(row_count * times, channels),
        preferred_element_type=jnp.float32,
    )
    part_imag = jnp.dot(
        folder,
        visibility_imag.reshape(row_count * times, channels),
        preferred_element_type=jnp.float32,
    )
    peak = jnp.maximum(
        jnp.max(jnp.abs(part_real), axis=1), jnp.max(jnp.abs(part_imag), axis=1)
    )
    step = lax.reduce_precision(jnp.maximum(peak, 1e-30) * (1.0078125 / 32767.0), 8, 7)
    invert = (1.0 / step)[:, None]
    code_real = jnp.round(part_real * invert).astype(jnp.int32)
    code_imag = jnp.round(part_imag * invert).astype(jnp.int32)
    packed = ((code_real << 16) | (code_imag & 65535)).reshape(owners, sent, channels)
    rank_row = jnp.broadcast_to(slot_rank[:, :, None], (owners, distinct, times))
    note = jnp.stack(
        [
            step.reshape(owners, sent),
            part_weight.reshape(owners, sent),
            rank_row.reshape(owners, sent).astype(jnp.float32),
        ],
        axis=1,
    )
    came_note = lax.all_to_all(note, "bl", split_axis=0, concat_axis=0, tiled=True)
    came = lax.all_to_all(packed, "bl", split_axis=0, concat_axis=0, tiled=True)

    came_step = came_note[:, 0].reshape(owners, distinct, times)
    came_weight = came_note[:, 1].reshape(owners, distinct, times)
    came_rank = came_note[:, 2].reshape(owners, distinct, times).astype(jnp.int32)
    time_id = jnp.arange(times, dtype=jnp.int32)
    group_id = jnp.arange(per_owner, dtype=jnp.int32)
    chosen = (came_rank[None, None] == group_id[None, :, None, None, None]) & (
        time_id[:, None, None, None, None] == time_id[None, None, None, None, :]
    )
    selector = (
        jnp.where(chosen, came_step[None, None], 0.0)
        .astype(jnp.bfloat16)
        .reshape(times * per_owner, owners * sent)
    )
    weight_sum = jnp.sum(jnp.where(chosen, came_weight[None, None], 0.0), axis=(2, 3, 4))
    scale = (1.0 / jnp.maximum(weight_sum, 1.0)).reshape(times * per_owner, 1)

    came = came.reshape(owners * sent, channels)
    real_high = (came >> 24).astype(jnp.bfloat16)
    real_low = ((came >> 16) & 255).astype(jnp.bfloat16)
    imag_code = (came << 16) >> 16
    imag_high = (imag_code >> 8).astype(jnp.bfloat16)
    imag_low = (imag_code & 255).astype(jnp.bfloat16)

    def gather(high, low):
        upper = jnp.dot(selector, high, preferred_element_type=jnp.float32)
        lower = jnp.dot(selector, low, preferred_element_type=jnp.float32)
        return 256.0 * upper + lower

    taper = taper_of(channels)[None, :]
    mean_real = gather(real_high, real_low) * scale * taper
    mean_imag = gather(imag_high, imag_low) * scale * taper
    short = channels // RADIX
    r = [mean_real[:, i * short : (i + 1) * short] for i in range(RADIX)]
    m = [mean_imag[:, i * short : (i + 1) * short] for i in range(RADIX)]
    er, ei, fr, fi = r[0] + r[2], m[0] + m[2], r[1] + r[3], m[1] + m[3]
    gr, gi, hr, hi = r[0] - r[2], m[0] - m[2], r[1] - r[3], m[1] - m[3]
    folded = jnp.stack(
        [
            jnp.concatenate([er + fr, ei + fi], axis=1),
            jnp.concatenate([gr + hi, gi - hr], axis=1),
            jnp.concatenate([er - fr, ei - fi], axis=1),
            jnp.concatenate([gr - hi, gi + hr], axis=1),
        ]
    )
    spectrum = jnp.einsum(
        "qnf,qfk->qnk", folded, dft_table(channels), precision=lax.Precision.HIGH
    ).reshape(RADIX, times, per_owner, 2 * short)
    size = lax.axis_size("tm")
    following = lax.ppermute(spectrum[:, 0], "tm", [(i, i - 1) for i in range(1, size)])
    pair = jnp.sum(spectrum[:, :-1] * spectrum[:, 1:], axis=1) + spectrum[:, -1] * following
    power = pair[..., :short] + pair[..., short:]
    rows = per_owner // parts
    power = power.reshape(RADIX, parts, rows, short).transpose(1, 2, 0, 3)
    me = lax.axis_index("tm")
    total = lax.dynamic_index_in_dim(power, me, 0, keepdims=False)
    for hop in range(1, parts):
        block = lax.dynamic_index_in_dim(power, lax.rem(me + hop, parts), 0, keepdims=False)
        route = [(i, (i + hop) % parts) for i in range(parts)]
        total = total + lax.ppermute(block, "tm", route)
    return total.transpose(0, 2, 1).reshape(rows, channels)


def solution(mesh):
    placed = (P("bl", "tm", None), P("bl", "tm", None), P("bl", "tm"), P("bl"), P())
    return jax.shard_map(
        per_device, mesh=mesh, in_specs=placed, out_specs=P(("bl", "tm"), None), check_vma=False
    )
```

time: 209 us -> 255 us (1.22)
  local copies, waits for them, and re-layouts: 7.98 us -> 127 us
  waiting for transfers between devices: 99.6 us -> 54.9 us
  matrix products: 32.7 us -> 14.1 us
  other arithmetic: 27.3 us -> 42.2 us
  between operations: 14.3 us -> 1.09 us
  starting transfers between devices: 25.7 us -> 15.5 us
    convert_element_type x3 -> x9, local copies, waits for them, and re-layouts: 0.77 us -> 114 us  [the longest x1 113 us: per_device(): folder = (hit[:, None, :, None] * (same_time[:, None, :] * weights[None])...]
    all_to_all x4 -> x2, waiting for transfers between devices: 74.1 us -> 42.2 us  [the longest x1 41.2 us: per_device(): came = lax.all_to_all(packed, 'bl', split_axis=0, concat_axis=0, tiled=True)]
    convert_element_type x2 -> x9, other arithmetic: 0.01 us -> 22.8 us  [the longest x1 20.7 us: per_device(): folder = (hit[:, None, :, None] * (same_time[:, None, :] * weights[None])...]
    mul x2 -> x3, other arithmetic: 19.6 us -> 0.06 us  [the longest x1 0.05 us: per_device(): same_time[:, None, :] * weights[None]]
    dot_general x6 -> x7, matrix products: 32.7 us -> 14.1 us  [the longest x1 5.99 us: per_device(): jnp.dot(folder, visibility_real.reshape(row_count * times, channels), pre...]
    reduce_scatter x1 -> x0, waiting for transfers between devices: 17.7 us -> none  [per_device(): lax.psum_scatter(partial_power, 'tm', scatter_dimension=0, tiled=True)]
    all_to_all x4 -> x2, starting transfers between devices: 21.4 us -> 10.7 us  [the longest x1 6.34 us: per_device(): lax.all_to_all(note, 'bl', split_axis=0, concat_axis=0, tiled=True)]
    reshape x0 -> x3, local copies, waits for them, and re-layouts: none -> 7.54 us  [the longest x1 3.74 us: per_device(): visibility_imag.reshape(row_count * times, channels)]
  transfers between devices with their start and end apart: 6 -> 6, of which waited for: 5 -> 6; matrix products, arithmetic and copies ran while one was open for 20% -> 6% of each run, Pallas kernels for 0% -> 0%
where the time goes in v1:
time: 255 us
  local copies, waits for them, and re-layouts  127 us (50%)
  waiting for transfers between devices  54.9 us (22%)
  other arithmetic  42.2 us (17%)
  starting transfers between devices  15.5 us (6%)
  matrix products  14.1 us (6%)
    convert_element_type x1, local copies, waits for them, and re-layouts, per_device(): folder = (hit[:, None, :, None] * (same_time[:, None, :] * weights[None])...  113 us
    all_to_all x1, waiting for transfers between devices, per_device(): came = lax.all_to_all(packed, 'bl', split_axis=0, concat_axis=0, tiled=True)  41.2 us
    convert_element_type x1, other arithmetic, per_device(): folder = (hit[:, None, :, None] * (same_time[:, None, :] * weights[None])...  20.7 us
    ppermute x1, waiting for transfers between devices, per_device(): lax.ppermute(spectrum[:, 0], 'tm', [(i, i - 1) for i in range(1, size)])  8.37 us
    all_to_all x1, starting transfers between devices, per_device(): lax.all_to_all(note, 'bl', split_axis=0, concat_axis=0, tiled=True)  6.34 us
    dot_general x1, matrix products, per_device(): jnp.dot(folder, visibility_real.reshape(row_count * times, channels), pre...  5.99 us
    neg x1, other arithmetic, dft_table(): top = jnp.concatenate([cosine, -sine], axis=2)  5.36 us
  transfers between devices with their start and end apart: 6, of which 6 were waited for; matrix products, arithmetic and copies ran while one was open for 6% of the time, Pallas kernels for 0%

profile of v1, /device:TPU:1, one launch (start us, length us, event | category | flops | bytes accessed | tf_op | source)
XLA Modules:
  0.0 255.0 jit_solution(11585225171885261629)
XLA Ops:
  0.0 0.7 fusion.49
  0.7 1.1 reduce-window.6
  2.1 0.8 fusion.48
  2.9 0.7 multiply_add_fusion
  3.5 0.9 select_reduce_fusion.1
  4.7 0.2 reduce_window_sum.30
  5.2 0.2 select_reduce_fusion
  5.5 0.8 copy.79
  6.4 0.9 multiply_reduce_fusion
  7.4 20.7 %multiply_convert_fusion = bf16[144,4,384,4]{3,2,1,0:T(8,128)(2,1)} fusion(s32[4,384,4]{2,1,0:T(8,128)S(1)} %broadcast_multiply_fusion, s32[144,384]{1,0:T(8,128)S(1)} %fusion.34), kind=kLoop, calls=%fused_computation | loop fusion | flops 1769472 | bytes 2015232 | tf_op jit(solution)/shard_map/convert_element_type | solution.py:81
  28.1 113.3 %convert_element_type.172 = bf16[576,1536]{1,0:T(8,128)(2,1)} reshape(bf16[144,4,384,4]{3,2,1,0:T(8,128)(2,1)} %multiply_convert_fusion) | data formatting | bytes 3538944 | tf_op jit(solution)/shard_map/convert_element_type | solution.py:81
  141.4 3.0 %reshape.408 = bf16[1536,1024]{1,0:T(8,128)(2,1)} reshape(bf16[384,4,1024]{2,1,0:T(4,128)(2,1)S(1)} %copy-done) | data formatting | bytes 6291456 | tf_op jit(solution)/shard_map/reshape | solution.py:87
  144.4 3.7 %reshape.409 = bf16[1536,1024]{1,0:T(8,128)(2,1)S(1)} reshape(bf16[384,4,1024]{2,1,0:T(4,128)(2,1)} %param.6) | data formatting | bytes 6291456 | tf_op jit(solution)/shard_map/reshape | solution.py:92
  148.2 6.0 %abs_reduce_fusion.1 = (f32[576]{0:T(1024)S(1)}, f32[576,1024]{1,0:T(8,128)}) fusion(bf16[576,1536]{1,0:T(8,128)(2,1)} %convert_element_type.172, bf16[1536,1024]{1,0:T(8,128)(2,1)} %reshape.408), kind=kOutput, calls=%fused_computation.16 | convolution fusion | flops 1813118464 | bytes 7276800 | tf_op jit(solution)/shard_map/dot_general | solution.py:85
  154.2 3.5 %abs_reduce_fusion = (f32[576]{0:T(1024)S(1)}, f32[576,1024]{1,0:T(8,128)}) fusion(bf16[576,1536]{1,0:T(8,128)(2,1)S(1)} %copy-done.1, bf16[1536,1024]{1,0:T(8,128)(2,1)S(1)} %reshape.409), kind=kOutput, calls=%fused_computation.15 | convolution fusion | flops 1813118464 | bytes 7276800 | tf_op jit(solution)/shard_map/dot_general | solution.py:90
  157.7 0.4 select_reduce_fusion.2
  158.4 0.7 reshape.416
  159.1 6.3 %all-to-all-start = ((f32[8,1,216]{2,1,0:T(1,128)}), f32[8,1,216]{2,1,0:T(1,128)S(1)}, u32[]{:S(2)}, u32[]{:S(2)}) async-start(f32[8,1,216]{2,1,0:T(1,128)} %reshape.416), calls=%async_computation | async-start | bytes 16384 | tf_op jit(solution)/shard_map/all_to_all | solution.py:112
  165.5 4.3 %and_or_fusion = s32[576,1024]{1,0:T(8,128)} fusion(f32[576,1024]{1,0:T(8,128)} %get-tuple-element.30, f32[576,1024]{1,0:T(8,128)} %get-tuple-element.28, f32[576]{0:T(1024)S(1)} %get-tuple-element.5), kind=kLoop, calls=%fused_computation.14 | loop fusion | flops 5308416 | bytes 7080192 | tf_op jit(solution)/shard_map/or | solution.py:102
  169.8 1.1 all-to-all-done
  170.8 4.4 %all-to-all-start.1 = ((s32[8,72,1024]{2,1,0:T(8,128)}), s32[8,72,1024]{2,1,0:T(8,128)S(1)}, u32[]{:S(2)}, u32[]{:S(2)}) async-start(s32[8,72,1024]{2,1,0:T(8,128)} %bitcast.88), calls=%async_computation.1 | async-start | bytes 4718592 | tf_op jit(solution)/shard_map/all_to_all | solution.py:113
  175.2 0.7 multiply_reduce_fusion.1
  176.7 5.4 %fusion.33 = (f32[4,256,256]{2,1,0:T(8,128)}, f32[4,256,256]{2,1,0:T(8,128)}, f32[4,256,256]{2,1,0:T(8,128)}) fusion(s32[4,256]{1,0:T(4,128)S(1)} %iota_add_fusion), kind=kLoop, calls=%fused_computation.63 | loop fusion | flops 3932160 | bytes 3149824 | tf_op jit(solution)/shard_map/neg | solution.py:31
  182.0 0.5 broadcast.341
  182.6 0.7 reduce.2
  183.9 0.2 iota_compare_fusion.2
  184.2 0.8 fusion.20
  185.0 0.4 convert_element_type.180
  185.6 0.8 fusion.21
  186.5 41.2 %all-to-all-done.1 = s32[8,72,1024]{2,1,0:T(8,128)S(1)} async-done(((s32[8,72,1024]{2,1,0:T(8,128)}), s32[8,72,1024]{2,1,0:T(8,128)S(1)}, u32[]{:S(2)}, u32[]{:S(2)}) %all-to-all-start.1) | async-done | bytes 2359328 | tf_op jit(solution)/shard_map/all_to_all | solution.py:113
  227.7 1.3 and_convert_fusion
  229.0 0.6 convolution_multiply_fusion
  229.6 0.6 fusion.19
  230.3 0.6 convolution_multiply_fusion.1
  230.9 0.6 fusion.17
  232.0 0.9 copy-done.2
  232.9 0.3 copy-done.3
  233.2 0.3 copy-done.4
  233.5 2.3 fusion
  235.9 4.2 %collective-permute-start = (f32[4,64,512]{2,1,0:T(8,128)S(1)}, f32[4,64,512]{2,1,0:T(8,128)S(1)}, u32[]{:S(2)}, u32[]{:S(2)}) collective-permute-start(f32[4,64,512]{2,1,0:T(8,128)S(1)} %slice_bitcast_fusion), channel_id=1, source_target_pairs={{1,0},{2,1},{3,2},{5,4},{6,5},{7,6},{9,8},{10,9},{11,10},{13,12},{... | collective-permute-start | bytes 1572872 | tf_op jit(solution)/shard_map/ppermute | solution.py:163
  240.2 0.3 fusion.15
  240.4 8.4 %collective-permute-done = f32[4,64,512]{2,1,0:T(8,128)S(1)} collective-permute-done((f32[4,64,512]{2,1,0:T(8,128)S(1)}, f32[4,64,512]{2,1,0:T(8,128)S(1)}, u32[]{:S(2)}, u32[]{:S(2)}) %collective-permute-start) | collective-permute-done | bytes 524320 | tf_op jit(solution)/shard_map/ppermute | solution.py:163
  249.2 0.4 collective-permute-start.3
  249.6 0.8 collective-permute-done.1
  250.4 1.9 collective-permute-done.2
  252.3 1.6 collective-permute-done.3
  253.9 0.2 copy.95
  254.1 0.8 copy.96
  (62 shorter events, 3.4 us)
Async XLA Ops:
  28.1 113.3 %copy-start = (bf16[384,4,1024]{2,1,0:T(4,128)(2,1)S(1)}, bf16[384,4,1024]{2,1,0:T(4,128)(2,1)}, u32[]{:S(2)}) copy-start(bf16[384,4,1024]{2,1,0:T(4,128)(2,1)} %param.5) | copy-start | bytes 9437188
  148.2 6.0 %copy-start.1 = (bf16[576,1536]{1,0:T(8,128)(2,1)S(1)}, bf16[576,1536]{1,0:T(8,128)(2,1)}, u32[]{:S(2)}) copy-start(bf16[576,1536]{1,0:T(8,128)(2,1)} %convert_element_type.172) | copy-start | bytes 5308420
  159.1 11.7 %all-to-all-start = ((f32[8,1,216]{2,1,0:T(1,128)}), f32[8,1,216]{2,1,0:T(1,128)S(1)}, u32[]{:S(2)}, u32[]{:S(2)}) async-start(f32[8,1,216]{2,1,0:T(1,128)} %reshape.416), calls=%async_computation | async-start | bytes 16384 | tf_op jit(solution)/shard_map/all_to_all | solution.py:112
  170.8 56.9 %all-to-all-start.1 = ((s32[8,72,1024]{2,1,0:T(8,128)}), s32[8,72,1024]{2,1,0:T(8,128)S(1)}, u32[]{:S(2)}, u32[]{:S(2)}) async-start(s32[8,72,1024]{2,1,0:T(8,128)} %bitcast.88), calls=%async_computation.1 | async-start | bytes 4718592 | tf_op jit(solution)/shard_map/all_to_all | solution.py:113
  231.7 1.2 copy-start.2
  231.7 1.5 copy-start.3
  231.7 1.8 copy-start.4
  235.9 12.9 %collective-permute-start = (f32[4,64,512]{2,1,0:T(8,128)S(1)}, f32[4,64,512]{2,1,0:T(8,128)S(1)}, u32[]{:S(2)}, u32[]{:S(2)}) collective-permute-start(f32[4,64,512]{2,1,0:T(8,128)S(1)} %slice_bitcast_fusion), channel_id=1, source_target_pairs={{1,0},{2,1},{3,2},{5,4},{6,5},{7,6},{9,8},{10,9},{11,10},{13,12},{... | collective-permute-start | bytes 1572872 | tf_op jit(solution)/shard_map/ppermute | solution.py:163
  249.0 1.4 collective-permute-start.1
  249.1 3.2 %collective-permute-start.2 = (f32[16,4,256]{2,0,1:T(8,128)S(1)}, f32[16,4,256]{2,0,1:T(8,128)S(1)}, u32[]{:S(2)}, u32[]{:S(2)}) collective-permute-start(f32[16,4,256]{2,0,1:T(8,128)S(1)} %get-tuple-element.21), channel_id=1, source_target_pairs={{0,2},{1,3},{2,0},{3,1},{4,6},{5,7},{6,4},{7,5},{8,10},{9,11},{10,... | collective-permute-start | bytes 196616 | tf_op jit(solution)/shard_map/ppermute | solution.py:173
  249.2 4.7 %collective-permute-start.3 = (f32[16,4,256]{2,0,1:T(8,128)S(1)}, f32[16,4,256]{2,0,1:T(8,128)S(1)}, u32[]{:S(2)}, u32[]{:S(2)}) collective-permute-start(f32[16,4,256]{2,0,1:T(8,128)S(1)} %get-tuple-element.20), channel_id=1, source_target_pairs={{0,3},{1,0},{2,1},{3,2},{4,7},{5,4},{6,5},{7,6},{8,11},{9,8},{10,9... | collective-permute-start | bytes 196616 | tf_op jit(solution)/shard_map/ppermute | solution.py:173

commit v2 on v1

--- a/solution.py
+++ b/solution.py
@@ -22,12 +22,23 @@
 
 def dft_table(channels):
     short = channels // RADIX
-    residue = jnp.arange(RADIX, dtype=jnp.int32)[:, None, None]
-    row = jnp.arange(short, dtype=jnp.int32)[None, :, None]
-    column = jnp.arange(short, dtype=jnp.int32)[None, None, :]
-    turns = row * (RADIX * column + residue) % channels
-    angle = 2.0 * math.pi / channels * turns.astype(jnp.float32)
-    cosine, sine = jnp.cos(angle), jnp.sin(angle)
+    fine = math.isqrt(short)
+    turn = 2.0 * math.pi / channels
+    delay = (
+        RADIX * jnp.arange(short, dtype=jnp.int32)[None, None, :]
+        + jnp.arange(RADIX, dtype=jnp.int32)[:, None, None]
+    )
+
+    def wave(rows):
+        angle = turn * (rows[None, :, None] * delay % channels).astype(jnp.float32)
+        return lax.optimization_barrier((jnp.cos(angle), jnp.sin(angle)))
+
+    coarse_cos, coarse_sin = wave(fine * jnp.arange(short // fine, dtype=jnp.int32))
+    fine_cos, fine_sin = wave(jnp.arange(fine, dtype=jnp.int32))
+    ac, as_ = coarse_cos[:, :, None, :], coarse_sin[:, :, None, :]
+    bc, bs = fine_cos[:, None], fine_sin[:, None]
+    cosine = (ac * bc - as_ * bs).reshape(RADIX, short, short)
+    sine = (as_ * bc + ac * bs).reshape(RADIX, short, short)
     top = jnp.concatenate([cosine, -sine], axis=2)
     bottom = jnp.concatenate([sine, cosine], axis=2)
     return jnp.concatenate([top, bottom], axis=1)
@@ -73,15 +84,13 @@
     row_slot, slot_rank = slots(labels, owner_of, owners, distinct)
 
     sent = distinct * times
-    slot_id = jnp.arange(owners * distinct, dtype=jnp.int32)
-    same_time = jnp.eye(times, dtype=jnp.int32)
-    hit = (row_slot[None, :] == slot_id[:, None]).astype(jnp.int32)
-    folder = (
-        (hit[:, None, :, None] * (same_time[:, None, :] * weights[None])[None])
-        .astype(jnp.bfloat16)
-        .reshape(owners * sent, row_count * times)
-    )
-    part_weight = jnp.sum(hit[:, :, None] * weights[None], axis=1).astype(jnp.float32)
+    slot_id = jnp.arange(owners * sent, dtype=jnp.int32)[:, None]
+    row_key = row_slot[:, None] * times + jnp.arange(times, dtype=jnp.int32)[None, :]
+    row_key = row_key.reshape(1, row_count * times)
+    row_weight = weights.astype(jnp.float32).reshape(1, row_count * times)
+    folder = jnp.where(slot_id == row_key, row_weight, 0.0)
+    part_weight = jnp.sum(folder, axis=1)
+    folder = folder.astype(jnp.bfloat16)
     part_real = jnp.dot(
         folder,
         visibility_real.reshape(row_count * times, channels),
@@ -112,20 +121,14 @@
     came_note = lax.all_to_all(note, "bl", split_axis=0, concat_axis=0, tiled=True)
     came = lax.all_to_all(packed, "bl", split_axis=0, concat_axis=0, tiled=True)
 
-    came_step = came_note[:, 0].reshape(owners, distinct, times)
-    came_weight = came_note[:, 1].reshape(owners, distinct, times)
-    came_rank = came_note[:, 2].reshape(owners, distinct, times).astype(jnp.int32)
-    time_id = jnp.arange(times, dtype=jnp.int32)
-    group_id = jnp.arange(per_owner, dtype=jnp.int32)
-    chosen = (came_rank[None, None] == group_id[None, :, None, None, None]) & (
-        time_id[:, None, None, None, None] == time_id[None, None, None, None, :]
-    )
-    selector = (
-        jnp.where(chosen, came_step[None, None], 0.0)
-        .astype(jnp.bfloat16)
-        .reshape(times * per_owner, owners * sent)
-    )
-    weight_sum = jnp.sum(jnp.where(chosen, came_weight[None, None], 0.0), axis=(2, 3, 4))
+    came_step = came_note[:, 0].reshape(1, owners * sent)
+    came_weight = came_note[:, 1].reshape(1, owners * sent)
+    came_rank = came_note[:, 2].reshape(1, owners * sent).astype(jnp.int32)
+    came_time = jnp.arange(owners * sent, dtype=jnp.int32)[None, :] % times
+    item = jnp.arange(times * per_owner, dtype=jnp.int32)[:, None]
+    chosen = item == came_time * per_owner + came_rank
+    selector = jnp.where(chosen, came_step, 0.0).astype(jnp.bfloat16)
+    weight_sum = jnp.sum(jnp.where(chosen, came_weight, 0.0), axis=1)
     scale = (1.0 / jnp.maximum(weight_sum, 1.0)).reshape(times * per_owner, 1)
 
     came = came.reshape(owners * sent, channels)

time: 255 us -> 124 us (0.49)
  local copies, waits for them, and re-layouts: 127 us -> 13.6 us
  other arithmetic: 42.2 us -> 17.1 us
  waiting for transfers between devices: 54.9 us -> 60.1 us
    convert_element_type x7 -> x2, local copies, waits for them, and re-layouts: 114 us -> 0.21 us  [the longest x1 0.14 us: per_device(): row_weight = weights.astype(jnp.float32).reshape(1, row_count * times)]
    convert_element_type x6 -> x2, other arithmetic: 21.5 us -> 0.72 us  [the longest x1 0.7 us: per_device(): row_weight = weights.astype(jnp.float32).reshape(1, row_count * times)]
    all_to_all x1, waiting for transfers between devices: 41.2 us -> 45.7 us  [per_device(): came = lax.all_to_all(packed, 'bl', split_axis=0, concat_axis=0, tiled=True)]
    neg x1, other arithmetic: 5.36 us -> 1.07 us  [dft_table(): top = jnp.concatenate([cosine, -sine], axis=2)]
  transfers between devices with their start and end apart: 6 -> 6, of which waited for: 6 -> 6; matrix products, arithmetic and copies ran while one was open for 6% -> 8% of each run, Pallas kernels for 0% -> 0%
where the time goes in v2:
time: 124 us; the launch traced here: 123 us
  waiting for transfers between devices  60.1 us (48%)
  other arithmetic  17.1 us (14%)
  matrix products  16.3 us (13%)
  starting transfers between devices  15.4 us (12%)
  local copies, waits for them, and re-layouts  13.6 us (11%)
    all_to_all x1, waiting for transfers between devices, per_device(): came = lax.all_to_all(packed, 'bl', split_axis=0, concat_axis=0, tiled=True)  45.7 us
    ppermute x1, waiting for transfers between devices, per_device(): lax.ppermute(spectrum[:, 0], 'tm', [(i, i - 1) for i in range(1, size)])  8.37 us
    all_to_all x1, starting transfers between devices, per_device(): lax.all_to_all(note, 'bl', split_axis=0, concat_axis=0, tiled=True)  6.34 us
    reshape x1, local copies, waits for them, and re-layouts, per_device(): visibility_real.reshape(row_count * times, channels)  5.53 us
    dot_general x1, matrix products, per_device(): jnp.dot(folder, visibility_real.reshape(row_count * times, channels), pre...  5.48 us
    dot_general x1, matrix products, per_device(): jnp.dot(folder, visibility_imag.reshape(row_count * times, channels), pre...  5.45 us
    ppermute x1, starting transfers between devices, per_device(): lax.ppermute(spectrum[:, 0], 'tm', [(i, i - 1) for i in range(1, size)])  4.69 us
    ppermute x3, waiting for transfers between devices, per_device(): total = total + lax.ppermute(block, 'tm', route)  4.27 us
  transfers between devices with their start and end apart: 6, of which 6 were waited for; matrix products, arithmetic and copies ran while one was open for 8% of the time, Pallas kernels for 0%

profile of v2, /device:TPU:1, one launch (start us, length us, event | category | flops | bytes accessed | tf_op | source)
XLA Modules:
  0.0 123.5 jit_solution(13567531950098955220)
XLA Ops:
  0.0 0.7 fusion.70
  0.7 1.1 reduce-window.6
  1.8 0.2 slice_reduce_fusion
  2.1 0.8 fusion.69
  2.9 0.7 multiply_add_fusion.1
  3.5 0.9 select_reduce_fusion.2
  4.4 0.2 fusion.28
  4.7 0.2 reduce_window_sum.30
  5.2 0.2 select_reduce_fusion.1
  5.7 0.7 convert_element_type.107
  6.5 0.1 broadcast_in_dim.101
  6.7 5.5 %reshape.274 = bf16[1536,1024]{1,0:T(8,128)(2,1)} reshape(bf16[384,4,1024]{2,1,0:T(4,128)(2,1)} %param.5) | data formatting | bytes 6291456 | tf_op jit(solution)/shard_map/reshape | solution.py:96
  12.2 0.5 select_reduce_fusion
  12.7 5.5 %abs_reduce_fusion.1 = (f32[576]{0:T(1024)S(1)}, f32[576,1024]{1,0:T(8,128)}) fusion(bf16[1536,1024]{1,0:T(8,128)(2,1)} %reshape.274, f32[1536]{0:T(1024)S(1)} %broadcast_in_dim.101, s32[1536]{0:T(1024)S(1)} %add.197), kind=kOutput, calls=%fused_computation.18 | convolution fusion | flops 1814887936 | bytes 5519616 | tf_op jit(solution)/shard_map/dot_general | solution.py:94
  18.2 3.0 %reshape.275 = bf16[1536,1024]{1,0:T(8,128)(2,1)} reshape(bf16[384,4,1024]{2,1,0:T(4,128)(2,1)S(1)} %copy-done) | data formatting | bytes 6291456 | tf_op jit(solution)/shard_map/reshape | solution.py:101
  21.2 5.4 %abs_reduce_fusion = (f32[576]{0:T(1024)S(1)}, f32[576,1024]{1,0:T(8,128)}) fusion(bf16[1536,1024]{1,0:T(8,128)(2,1)} %reshape.275, f32[1536]{0:T(1024)S(1)} %broadcast_in_dim.101, s32[1536]{0:T(1024)S(1)} %add.197), kind=kOutput, calls=%fused_computation.17 | convolution fusion | flops 1814887936 | bytes 5519616 | tf_op jit(solution)/shard_map/dot_general | solution.py:99
  26.7 0.4 select_reduce_fusion.4
  27.3 0.7 reshape.301
  28.0 6.3 %all-to-all-start = ((f32[8,1,216]{2,1,0:T(1,128)}), f32[8,1,216]{2,1,0:T(1,128)S(1)}, u32[]{:S(2)}, u32[]{:S(2)}) async-start(f32[8,1,216]{2,1,0:T(1,128)} %reshape.301), calls=%async_computation | async-start | bytes 16384 | tf_op jit(solution)/shard_map/all_to_all | solution.py:121
  34.3 3.6 %and_or_fusion = s32[576,1024]{1,0:T(8,128)} fusion(f32[576,1024]{1,0:T(8,128)} %get-tuple-element.41, f32[576,1024]{1,0:T(8,128)S(1)} %copy-done.1, f32[576]{0:T(1024)S(1)} %get-tuple-element.15), kind=kLoop, calls=%fused_computation.16 | loop fusion | flops 5308416 | bytes 7080192 | tf_op jit(solution)/shard_map/or | solution.py:111
  37.9 1.8 %all-to-all-done = f32[8,1,216]{2,1,0:T(1,128)S(1)} async-done(((f32[8,1,216]{2,1,0:T(1,128)}), f32[8,1,216]{2,1,0:T(1,128)S(1)}, u32[]{:S(2)}, u32[]{:S(2)}) %all-to-all-start) | async-done | bytes 6944 | tf_op jit(solution)/shard_map/all_to_all | solution.py:121
  39.7 3.8 %all-to-all-start.1 = ((s32[8,72,1024]{2,1,0:T(8,128)}), s32[8,72,1024]{2,1,0:T(8,128)S(1)}, u32[]{:S(2)}, u32[]{:S(2)}) async-start(s32[8,72,1024]{2,1,0:T(8,128)} %bitcast.77), calls=%async_computation.1 | async-start | bytes 4718592 | tf_op jit(solution)/shard_map/all_to_all | solution.py:122
  43.5 0.7 multiply_reduce_fusion
  44.9 0.6 fusion.66
  45.5 1.3 %multiply_add_fusion = (f32[4,16,16,256]{3,2,1,0:T(8,128)S(1)}, f32[4,16,16,256]{3,2,1,0:T(8,128)}) fusion(f32[4,16,256]{2,1,0:T(8,128)S(1)} %get-tuple-element.12, f32[4,16,256]{2,1,0:T(8,128)S(1)} %get-tuple-element.11, f32[4,16,256]{2,1,0:T(8,128)S(1)} %get-tuple-element.10, f32[4,16,256]{2,1,0:T(8,128)S(1)} %get-tuple-element.9), kind=kLoop, calls=%fused_computation.44 | loop fusion | flops 1572864 | bytes 2359296 | tf_op jit(solution)/shard_map/add | solution.py:41
  46.8 1.1 bitcast_negate_fusion
  47.9 0.5 broadcast.280
  48.4 0.7 reduce.14
  49.4 0.2 select_reduce_fusion.3
  49.7 45.7 %all-to-all-done.1 = s32[8,72,1024]{2,1,0:T(8,128)S(1)} async-done(((s32[8,72,1024]{2,1,0:T(8,128)}), s32[8,72,1024]{2,1,0:T(8,128)S(1)}, u32[]{:S(2)}, u32[]{:S(2)}) %all-to-all-start.1) | async-done | bytes 2359328 | tf_op jit(solution)/shard_map/all_to_all | solution.py:122
  95.4 1.3 %and_convert_fusion = (bf16[8,72,1024]{2,1,0:T(8,128)(2,1)S(1)}, bf16[8,72,1024]{2,1,0:T(8,128)(2,1)S(1)}, bf16[8,72,1024]{2,1,0:T(8,128)(2,1)S(1)}, bf16[8,72,1024]{2,1,0:T(8,128)(2,1)S(1)}) fusion(s32[8,72,1024]{2,1,0:T(8,128)S(1)} %all-to-all-done.1), kind=kLoop, calls=%fused_computation.11 | loop fusion | flops 6488064 | bytes 7077888 | tf_op jit(solution)/shard_map/convert_element_type | solution.py:139
  96.7 0.8 convolution_multiply_fusion
  97.5 0.8 fusion.27
  98.3 0.8 convolution_multiply_fusion.1
  99.1 0.8 fusion.25
  100.4 0.9 copy-done.2
  101.4 0.3 copy-done.3
  101.7 2.3 %fusion = f32[4,256,512]{2,1,0:T(8,128)S(1)} fusion(f32[4,256,256]{2,1,0:T(8,128)S(1)} %bitcast.89, f32[4,256,256]{2,1,0:T(8,128)S(1)} %bitcast.83, f32[4,256,256]{2,1,0:T(8,128)S(1)} %copy-done.3, f32[1,256,512]{2,1,0:T(8,128)S(1)} %get-tuple-element.43, f32[1,256,512]{2,1,0:T(8,128)S(1)} %get-tuple-element.45, f32[1,256,512]{2,1,0:T(8,128)S(1)} %get-tuple-element.42, ...), kind=kOutput, calls=%fused_computation.2 | convolution fusion | flops 1615331328 | bytes 7340032 | tf_op jit(solution)/shard_map/qnf,qfk->qnk/dot_general | solution.py:162
  104.0 4.7 %collective-permute-start = (f32[4,64,512]{2,1,0:T(8,128)S(1)}, f32[4,64,512]{2,1,0:T(8,128)S(1)}, u32[]{:S(2)}, u32[]{:S(2)}) collective-permute-start(f32[4,64,512]{2,1,0:T(8,128)S(1)} %slice_bitcast_fusion), channel_id=1, source_target_pairs={{1,0},{2,1},{3,2},{5,4},{6,5},{7,6},{9,8},{10,9},{11,10},{13,12},{... | collective-permute-start | bytes 1572872 | tf_op jit(solution)/shard_map/ppermute | solution.py:166
  108.7 0.3 fusion.23
  109.0 8.4 %collective-permute-done = f32[4,64,512]{2,1,0:T(8,128)S(1)} collective-permute-done((f32[4,64,512]{2,1,0:T(8,128)S(1)}, f32[4,64,512]{2,1,0:T(8,128)S(1)}, u32[]{:S(2)}, u32[]{:S(2)}) %collective-permute-start) | collective-permute-done | bytes 524320 | tf_op jit(solution)/shard_map/ppermute | solution.py:166
  117.4 0.2 fusion.30
  117.7 0.4 collective-permute-start.3
  118.2 0.8 collective-permute-done.1
  119.0 1.9 %collective-permute-done.2 = f32[16,4,256]{2,0,1:T(8,128)S(1)} collective-permute-done((f32[16,4,256]{2,0,1:T(8,128)S(1)}, f32[16,4,256]{2,0,1:T(8,128)S(1)}, u32[]{:S(2)}, u32[]{:S(2)}) %collective-permute-start.2) | collective-permute-done | bytes 65568 | tf_op jit(solution)/shard_map/ppermute | solution.py:176
  120.8 1.6 %collective-permute-done.3 = f32[16,4,256]{2,0,1:T(8,128)S(1)} collective-permute-done((f32[16,4,256]{2,0,1:T(8,128)S(1)}, f32[16,4,256]{2,0,1:T(8,128)S(1)}, u32[]{:S(2)}, u32[]{:S(2)}) %collective-permute-start.3) | collective-permute-done | bytes 65568 | tf_op jit(solution)/shard_map/ppermute | solution.py:176
  122.5 0.2 copy.41
  122.7 0.8 copy.42
  (52 shorter events, 2.2 us)
Async XLA Ops:
  12.7 5.5 %copy-start = (bf16[384,4,1024]{2,1,0:T(4,128)(2,1)S(1)}, bf16[384,4,1024]{2,1,0:T(4,128)(2,1)}, u32[]{:S(2)}) copy-start(bf16[384,4,1024]{2,1,0:T(4,128)(2,1)} %param.6) | copy-start | bytes 9437188
  21.2 13.2 %copy-start.1 = (f32[576,1024]{1,0:T(8,128)S(1)}, f32[576,1024]{1,0:T(8,128)}, u32[]{:S(2)}) copy-start(f32[576,1024]{1,0:T(8,128)} %get-tuple-element.39) | copy-start | bytes 7077892
  28.0 11.7 %all-to-all-start = ((f32[8,1,216]{2,1,0:T(1,128)}), f32[8,1,216]{2,1,0:T(1,128)S(1)}, u32[]{:S(2)}, u32[]{:S(2)}) async-start(f32[8,1,216]{2,1,0:T(1,128)} %reshape.301), calls=%async_computation | async-start | bytes 16384 | tf_op jit(solution)/shard_map/all_to_all | solution.py:121
  39.7 55.7 %all-to-all-start.1 = ((s32[8,72,1024]{2,1,0:T(8,128)}), s32[8,72,1024]{2,1,0:T(8,128)S(1)}, u32[]{:S(2)}, u32[]{:S(2)}) async-start(s32[8,72,1024]{2,1,0:T(8,128)} %bitcast.77), calls=%async_computation.1 | async-start | bytes 4718592 | tf_op jit(solution)/shard_map/all_to_all | solution.py:122
  100.1 1.2 copy-start.2
  100.1 1.5 %copy-start.3 = (f32[4,256,256]{2,1,0:T(8,128)S(1)}, f32[4,256,256]{2,1,0:T(8,128)}, u32[]{:S(2)}) copy-start(f32[4,256,256]{2,1,0:T(8,128)} %bitcast_negate_fusion) | copy-start | bytes 3145732
  104.0 13.4 %collective-permute-start = (f32[4,64,512]{2,1,0:T(8,128)S(1)}, f32[4,64,512]{2,1,0:T(8,128)S(1)}, u32[]{:S(2)}, u32[]{:S(2)}) collective-permute-start(f32[4,64,512]{2,1,0:T(8,128)S(1)} %slice_bitcast_fusion), channel_id=1, source_target_pairs={{1,0},{2,1},{3,2},{5,4},{6,5},{7,6},{9,8},{10,9},{11,10},{13,12},{... | collective-permute-start | bytes 1572872 | tf_op jit(solution)/shard_map/ppermute | solution.py:166
  117.6 1.4 %collective-permute-start.1 = (f32[16,4,256]{2,0,1:T(8,128)S(1)}, f32[16,4,256]{2,0,1:T(8,128)S(1)}, u32[]{:S(2)}, u32[]{:S(2)}) collective-permute-start(f32[16,4,256]{2,0,1:T(8,128)S(1)} %get-tuple-element.29), channel_id=1, source_target_pairs={{0,1},{1,2},{2,3},{3,0},{4,5},{5,6},{6,7},{7,4},{8,9},{9,10},{10,1... | collective-permute-start | bytes 196616 | tf_op jit(solution)/shard_map/ppermute | solution.py:176
  117.7 3.2 %collective-permute-start.2 = (f32[16,4,256]{2,0,1:T(8,128)S(1)}, f32[16,4,256]{2,0,1:T(8,128)S(1)}, u32[]{:S(2)}, u32[]{:S(2)}) collective-permute-start(f32[16,4,256]{2,0,1:T(8,128)S(1)} %get-tuple-element.31), channel_id=1, source_target_pairs={{0,2},{1,3},{2,0},{3,1},{4,6},{5,7},{6,4},{7,5},{8,10},{9,11},{10,... | collective-permute-start | bytes 196616 | tf_op jit(solution)/shard_map/ppermute | solution.py:176
  117.7 4.7 %collective-permute-start.3 = (f32[16,4,256]{2,0,1:T(8,128)S(1)}, f32[16,4,256]{2,0,1:T(8,128)S(1)}, u32[]{:S(2)}, u32[]{:S(2)}) collective-permute-start(f32[16,4,256]{2,0,1:T(8,128)S(1)} %get-tuple-element.30), channel_id=1, source_target_pairs={{0,3},{1,0},{2,1},{3,2},{4,7},{5,4},{6,5},{7,6},{8,11},{9,8},{10,9... | collective-permute-start | bytes 196616 | tf_op jit(solution)/shard_map/ppermute | solution.py:176

commit v3 on v2

--- a/solution.py
+++ b/solution.py
@@ -1,8 +1,11 @@
+import functools
 import math
 
 import jax
 import jax.numpy as jnp
 from jax import lax
+from jax.experimental import pallas as pl
+from jax.experimental.pallas import tpu as pltpu
 from jax.sharding import PartitionSpec as P
 
 HARRIS = (0.35875, 0.48829, 0.14128, 0.01168)
@@ -71,6 +74,150 @@
         jnp.where(slot_hit, jnp.arange(per_owner, dtype=jnp.int32)[None, :, None], 0), axis=1
     )
     return row_slot, slot_rank
+
+
+def greet(axis, size):
+    me = lax.axis_index(axis)
+    barrier = pltpu.get_barrier_semaphore()
+    for hop in range(1, size):
+        pl.semaphore_signal(
+            barrier,
+            inc=1,
+            device_id={axis: lax.rem(me + hop, size)},
+            device_id_type=pl.DeviceIdType.MESH,
+        )
+    pl.semaphore_wait(barrier, size - 1)
+    return me
+
+
+def exchange_kernel(size, data, note, data_out, note_out, held, kept, sends, arrivals, local):
+    me = greet("bl", size)
+    copies = []
+    for which, (source, target) in enumerate(((note, note_out), (data, data_out))):
+        for hop in range(1, size):
+            peer = lax.rem(me + hop, size)
+            copy = pltpu.make_async_remote_copy(
+                src_ref=source.at[peer],
+                dst_ref=target.at[me],
+                send_sem=sends.at[which, hop - 1],
+                recv_sem=arrivals.at[which, hop - 1],
+                device_id={"bl": peer},
+                device_id_type=pl.DeviceIdType.MESH,
+            )
+            copy.start()
+            copies.append(copy)
+    inward = [
+        pltpu.make_async_copy(data.at[me], held, local.at[0]),
+        pltpu.make_async_copy(note.at[me], kept, local.at[1]),
+    ]
+    outward = [
+        pltpu.make_async_copy(held, data_out.at[me], local.at[0]),
+        pltpu.make_async_copy(kept, note_out.at[me], local.at[1]),
+    ]
+    for copy in inward:
+        copy.start()
+    for copy in inward:
+        copy.wait()
+    for copy in outward:
+        copy.start()
+    for copy in outward:
+        copy.wait()
+    for copy in copies:
+        copy.wait()
+
+
+def exchange(data, note):
+    size = data.shape[0]
+    anywhere = pl.BlockSpec(memory_space=pl.ANY)
+    return pl.pallas_call(
+        functools.partial(exchange_kernel, size),
+        out_shape=[
+            jax.ShapeDtypeStruct(data.shape, data.dtype),
+            jax.ShapeDtypeStruct(note.shape, note.dtype),
+        ],
+        in_specs=[anywhere, anywhere],
+        out_specs=[anywhere, anywhere],
+        scratch_shapes=[
+            pltpu.VMEM(data.shape[1:], data.dtype),
+            pltpu.VMEM(note.shape[1:], note.dtype),
+            pltpu.SemaphoreType.DMA((2, size - 1)),
+            pltpu.SemaphoreType.DMA((2, size - 1)),
+            pltpu.SemaphoreType.DMA((2,)),
+        ],
+        compiler_params=pltpu.CompilerParams(collective_id=0, has_side_effects=True),
+        cost_estimate=pl.CostEstimate(
+            flops=0, bytes_accessed=32 * data.size, transcendentals=0
+        ),
+    )(data, note)
+
+
+def tail_kernel(size, spectrum, out, following, share, came, sends, arrivals, step_sems):
+    radix, times, groups, width = spectrum.shape
+    short = width // 2
+    rows = groups // size
+    me = greet("tm", size)
+    ahead = pltpu.make_async_remote_copy(
+        src_ref=spectrum.at[:, 0],
+        dst_ref=following,
+        send_sem=step_sems.at[0],
+        recv_sem=step_sems.at[1],
+        device_id={"tm": lax.rem(me + size - 1, size)},
+        device_id_type=pl.DeviceIdType.MESH,
+    )
+    ahead.start()
+    for q in range(radix):
+        pair = spectrum[q, 0] * spectrum[q, 1]
+        for t in range(1, times - 1):
+            pair += spectrum[q, t] * spectrum[q, t + 1]
+        power = pair[:, :short] + pair[:, short:]
+        for p in range(size):
+            share[p, q] = power[p * rows : (p + 1) * rows]
+    ahead.wait()
+    for q in range(radix):
+        pair = spectrum[q, times - 1] * following[q]
+        power = pair[:, :short] + pair[:, short:]
+        power = jnp.where(me < size - 1, power, 0.0)
+        for p in range(size):
+            share[p, q] += power[p * rows : (p + 1) * rows]
+    copies = []
+    for hop in range(1, size):
+        peer = lax.rem(me + hop, size)
+        copy = pltpu.make_async_remote_copy(
+            src_ref=share.at[peer],
+            dst_ref=came.at[hop - 1],
+            send_sem=sends.at[hop - 1],
+            recv_sem=arrivals.at[hop - 1],
+            device_id={"tm": peer},
+            device_id_type=pl.DeviceIdType.MESH,
+        )
+        copy.start()
+        copies.append(copy)
+    total = share[me]
+    for hop, copy in enumerate(copies):
+        copy.wait()
+        total += came[hop]
+    out[...] = total
+
+
+def tail(spectrum, size):
+    radix, times, groups, width = spectrum.shape
+    block = (radix, groups // size, width // 2)
+    inside = pl.BlockSpec(memory_space=pltpu.VMEM)
+    return pl.pallas_call(
+        functools.partial(tail_kernel, size),
+        out_shape=jax.ShapeDtypeStruct(block, jnp.float32),
+        in_specs=[inside],
+        out_specs=inside,
+        scratch_shapes=[
+            pltpu.VMEM((radix, groups, width), jnp.float32),
+            pltpu.VMEM((size,) + block, jnp.float32),
+            pltpu.VMEM((size - 1,) + block, jnp.float32),
+            pltpu.SemaphoreType.DMA((size - 1,)),
+            pltpu.SemaphoreType.DMA((size - 1,)),
+            pltpu.SemaphoreType.DMA((2,)),
+        ],
+        compiler_params=pltpu.CompilerParams(collective_id=1, has_side_effects=True),
+    )(spectrum)
 
 
 def per_device(visibility_real, visibility_imag, weights, labels, owner_of):
@@ -118,8 +265,9 @@
         ],
         axis=1,
     )
-    came_note = lax.all_to_all(note, "bl", split_axis=0, concat_axis=0, tiled=True)
-    came = lax.all_to_all(packed, "bl", split_axis=0, concat_axis=0, tiled=True)
+    note = jnp.pad(note, ((0, 0), (0, 5), (0, -sent % 128)))
+    came, came_note = exchange(packed, note)
+    came_note = came_note[:, :, :sent]
 
     came_step = came_note[:, 0].reshape(1, owners * sent)
     came_weight = came_note[:, 1].reshape(1, owners * sent)
@@ -162,19 +310,8 @@
     spectrum = jnp.einsum(
         "qnf,qfk->qnk", folded, dft_table(channels), precision=lax.Precision.HIGH
     ).reshape(RADIX, times, per_owner, 2 * short)
-    size = lax.axis_size("tm")
-    following = lax.ppermute(spectrum[:, 0], "tm", [(i, i - 1) for i in range(1, size)])
-    pair = jnp.sum(spectrum[:, :-1] * spectrum[:, 1:], axis=1) + spectrum[:, -1] * following
-    power = pair[..., :short] + pair[..., short:]
-    rows = per_owner // parts
-    power = power.reshape(RADIX, parts, rows, short).transpose(1, 2, 0, 3)
-    me = lax.axis_index("tm")
-    total = lax.dynamic_index_in_dim(power, me, 0, keepdims=False)
-    for hop in range(1, parts):
-        block = lax.dynamic_index_in_dim(power, lax.rem(me + hop, parts), 0, keepdims=False)
-        route = [(i, (i + hop) % parts) for i in range(parts)]
-        total = total + lax.ppermute(block, "tm", route)
-    return total.transpose(0, 2, 1).reshape(rows, channels)
+    total = tail(spectrum, parts)
+    return total.transpose(1, 2, 0).reshape(per_owner // parts, channels)
 
 
 def solution(mesh):

time: 124 us -> 122 us (0.984)
  the two profiles are of different devices: /device:TPU:1 before, /device:TPU:11 now
where the time goes in v3:
time: 122 us; the launch traced here: 121 us
  Pallas kernels  71.7 us (59%)
  matrix products  19.8 us (16%)
  other arithmetic  16.3 us (13%)
  local copies, waits for them, and re-layouts  12.7 us (10%)
    pallas_call x1, Pallas kernels, exchange(): pl.pallas_call(functools.partial(exchange_kernel, size), out_shape=[jax.S...  56.5 us
    pallas_call x1, Pallas kernels, tail(): pl.pallas_call(functools.partial(tail_kernel, size), out_shape=jax.ShapeD...  15.2 us
    reshape x1, local copies, waits for them, and re-layouts, per_device(): visibility_real.reshape(row_count * times, channels)  5.53 us
    dot_general x1, matrix products, per_device(): jnp.dot(folder, visibility_real.reshape(row_count * times, channels), pre...  5.47 us
    dot_general x1, matrix products, per_device(): jnp.dot(folder, visibility_imag.reshape(row_count * times, channels), pre...  4.12 us
    convert_element_type x1, other arithmetic, per_device(): imag_low = (imag_code & 255).astype(jnp.bfloat16)  3.97 us
    dot_general x2, matrix products, gather(): upper = jnp.dot(selector, high, preferred_element_type=jnp.float32)  3.81 us
    dot_general x1, matrix products, per_device(): jnp.einsum('qnf,qfk->qnk', folded, dft_table(channels), precision=lax.Pre...  3.64 us

profile of v3, /device:TPU:11, one launch (start us, length us, event | category | flops | bytes accessed | tf_op | source)
XLA Modules:
  0.0 121.5 jit_solution(5383760016451560581)
XLA Ops:
  0.0 0.7 fusion.64
  0.7 1.1 reduce-window.6
  1.8 0.2 slice_reduce_fusion
  2.1 0.8 fusion.63
  2.8 0.7 multiply_add_fusion.1
  3.5 0.9 select_reduce_fusion.2
  4.4 0.2 fusion.27
  4.6 0.1 reshape.276
  4.7 0.2 reduce_window_sum.30
  4.9 0.1 reduce_window_sum.31
  5.1 0.1 add.157
  5.2 0.2 select_reduce_fusion.1
  5.4 0.1 iota_add_fusion
  5.6 0.1 add.162
  5.7 0.7 convert_element_type.109
  6.4 0.1 copy.10
  6.5 0.1 broadcast_in_dim.101
  6.7 5.5 %reshape.271 = bf16[1536,1024]{1,0:T(8,128)(2,1)} reshape(bf16[384,4,1024]{2,1,0:T(4,128)(2,1)} %param.5) | data formatting | bytes 6291456 | tf_op jit(solution)/shard_map/reshape | solution.py:243
  12.2 5.5 %abs_reduce_fusion.1 = (f32[576]{0:T(1024)S(1)}, f32[576,1024]{1,0:T(8,128)}) fusion(bf16[1536,1024]{1,0:T(8,128)(2,1)} %reshape.271, f32[1536]{0:T(1024)S(1)} %broadcast_in_dim.101, s32[1536]{0:T(1024)S(1)} %add.162), kind=kOutput, calls=%fused_computation.18 | convolution fusion | flops 1814887936 | bytes 5519616 | tf_op jit(solution)/shard_map/dot_general | solution.py:241
  17.7 3.0 %reshape.272 = bf16[1536,1024]{1,0:T(8,128)(2,1)} reshape(bf16[384,4,1024]{2,1,0:T(4,128)(2,1)S(1)} %copy-done) | data formatting | bytes 6291456 | tf_op jit(solution)/shard_map/reshape | solution.py:248
  20.7 4.1 %abs_reduce_fusion = (f32[576]{0:T(1024)S(1)}, f32[576,1024]{1,0:T(8,128)S(1)}) fusion(bf16[1536,1024]{1,0:T(8,128)(2,1)} %reshape.272, f32[1536]{0:T(1024)S(1)} %broadcast_in_dim.101, s32[1536]{0:T(1024)S(1)} %add.162), kind=kOutput, calls=%fused_computation.17 | convolution fusion | flops 1814887936 | bytes 5519616 | tf_op jit(solution)/shard_map/dot_general | solution.py:246
  24.8 1.9 %and_or_fusion = s32[576,1024]{1,0:T(8,128)} fusion(f32[576,1024]{1,0:T(8,128)S(1)} %get-tuple-element.42, f32[576,1024]{1,0:T(8,128)S(1)} %copy-done.1, f32[576]{0:T(1024)S(1)} %get-tuple-element.19), kind=kLoop, calls=%fused_computation.16 | loop fusion | flops 5308416 | bytes 7080192 | tf_op jit(solution)/shard_map/or | solution.py:258
  26.8 0.1 reduce_precision.18
  26.9 0.4 select_reduce_fusion.4
  27.3 0.5 select_reduce_fusion
  27.8 0.1 stack_reshape.4
  27.9 0.6 select_maximum_fusion.note
  28.5 56.5 %shard_map.55 = (s32[8,72,1024]{2,1,0:T(8,128)}, f32[8,8,128]{2,1,0:T(8,128)}) custom-call(s32[8,72,1024]{2,1,0:T(8,128)} %bitcast.35, f32[8,8,128]{2,1,0:T(8,128)} %select_maximum_fusion.note), custom_call_target="tpu_custom_call" | custom-call | bytes 18874368 | tf_op jit(solution)/shard_map/pallas_call | solution.py:132
  85.0 4.0 %and_convert_fusion = (bf16[8,72,1024]{2,1,0:T(8,128)(2,1)S(1)}, bf16[8,72,1024]{2,1,0:T(8,128)(2,1)}, bf16[8,72,1024]{2,1,0:T(8,128)(2,1)S(1)}, bf16[8,72,1024]{2,1,0:T(8,128)(2,1)S(1)}) fusion(s32[8,72,1024]{2,1,0:T(8,128)} %get-tuple-element.12), kind=kLoop, calls=%fused_computation.11 | loop fusion | flops 6488064 | bytes 7077888 | tf_op jit(solution)/shard_map/convert_element_type | solution.py:287
  89.0 0.8 convert_reduce_fusion
  89.8 0.1 convert_element_type.116
  89.9 0.9 slice_reduce_fusion.1
  90.7 0.1 broadcast_in_dim.107
  90.8 3.0 %convolution_multiply_fusion = f32[256,1024]{1,0:T(8,128)} fusion(bf16[576,1024]{1,0:T(8,128)(2,1)} %bitcast.42, bf16[576]{0:T(1024)(128)(2,1)S(1)} %broadcast_in_dim.107, s32[576]{0:T(1024)S(1)} %fusion.66), kind=kOutput, calls=%fused_computation.35 | convolution fusion | flops 302546944 | bytes 2231680 | tf_op jit(solution)/shard_map/dot_general | solution.py:290
  93.9 0.2 select_reduce_fusion.3
  94.2 0.7 multiply_reduce_fusion
  95.6 2.0 %fusion.26 = f32[256,1024]{1,0:T(8,128)S(1)} fusion(f32[256,1024]{1,0:T(8,128)} %convolution_multiply_fusion, bf16[576,1024]{1,0:T(8,128)(2,1)S(1)} %bitcast.37, f32[1024]{0:T(1024)S(1)} %fusion.79, f32[256]{0:T(256)S(1)} %maximum_divide_fusion, bf16[576]{0:T(1024)(128)(2,1)S(1)} %broadcast_in_dim.107, s32[576]{0:T(1024)S(1)} %fusion.66), kind=kOutput, calls=%fused_computation.41 | convolution fusion | flops 303071232 | bytes 3285376 | tf_op jit(solution)/shard_map/dot_general | solution.py:291
  97.7 0.8 convolution_multiply_fusion.1
  98.5 0.8 fusion.24
  99.3 0.1 maximum_bitcast_fusion
  99.5 0.1 fusion.43
  99.6 0.1 maximum_bitcast_fusion.1
  99.8 0.6 fusion.60
  100.3 0.3 multiply_add_fusion
  100.7 3.6 %fusion = f32[4,256,512]{2,1,0:T(8,128)} fusion(f32[4,256,256]{2,1,0:T(8,128)S(1)} %bitcast.43, f32[4,256,256]{2,1,0:T(8,128)S(1)} %bitcast.38, f32[4,256,256]{2,1,0:T(8,128)S(1)} %bitcast_negate_fusion, f32[1,256,512]{2,1,0:T(8,128)S(1)} %get-tuple-element.44, f32[1,256,512]{2,1,0:T(8,128)S(1)} %get-tuple-element.46, ...), kind=kOutput, calls=%fused_computation.2 | convolution fusion | flops 1615331328 | bytes 7340032 | tf_op jit(solution)/shard_map/qnf,qfk->qnk/dot_general | solution.py:310
  104.4 15.2 %shard_map.56 = f32[4,16,256]{2,1,0:T(8,128)} custom-call(f32[4,4,64,512]{3,2,1,0:T(8,128)} %bitcast.40), custom_call_target="tpu_custom_call" | custom-call | tf_op jit(solution)/shard_map/pallas_call | solution.py:206
  119.6 1.1 copy.12
  120.7 0.8 copy.13
  (27 shorter events, 0.6 us)
Async XLA Ops:
  12.2 5.5 %copy-start = (bf16[384,4,1024]{2,1,0:T(4,128)(2,1)S(1)}, bf16[384,4,1024]{2,1,0:T(4,128)(2,1)}, u32[]{:S(2)}) copy-start(bf16[384,4,1024]{2,1,0:T(4,128)(2,1)} %param.6) | copy-start | bytes 9437188
  20.7 4.1 %copy-start.1 = (f32[576,1024]{1,0:T(8,128)S(1)}, f32[576,1024]{1,0:T(8,128)}, u32[]{:S(2)}) copy-start(f32[576,1024]{1,0:T(8,128)} %get-tuple-element.40) | copy-start | bytes 7077892
